TPU v7x, 256 devices: a whole 4x4x8 slice. The times are simulated.
256 devices in a mesh: row: 16 (over z, y_hi), col: 8 (over x, core), depth: 2 (over y_lo).
Axes of the slice: x: 4, y: 4 (y_hi: 2, y_lo: 2; y = y_hi * 2 + y_lo), z: 8, core: 2. Of those that a mesh axis runs over, the one named last changes fastest.
Arguments:
- heads_concat: bfloat16 [8192, 16384], P('row', ('depth', 'col')), may hold values from -6 to 6
- w_out: bfloat16 [16384, 7168], P(('depth', 'row'), 'col'), may hold values from -0.046875 to 0.046875
Outputs:
- projected: bfloat16 [8192, 7168], P('row', ('col', 'depth'))
All inputs are finite; a program needn't handle non-finite values.
Results may differ from a plain program's by a relative error of at most 0.001.
Values may be sent and summed in bfloat16 or wider, within the bound.
A program may use at most 128 MiB of HBM per device.

v0:
```python
import jax
import jax.numpy as jnp
from jax import lax
from jax.sharding import PartitionSpec as P


def from_everyone(array, axis):
    copies = jnp.broadcast_to(array, (lax.axis_size(axis), *array.shape))
    return lax.all_to_all(copies, axis, split_axis=0, concat_axis=0, tiled=True)


def joined_along(tiles, dim):
    tiles = jnp.moveaxis(tiles, 0, dim)
    shape = tiles.shape
    return tiles.reshape(*shape[:dim], shape[dim] * shape[dim + 1], *shape[dim + 2 :])


def collect(array, axis, dim):
    tiles = from_everyone(array, axis)
    return joined_along(tiles, dim)


def in_blocks(array, dim, size):
    shape = array.shape
    tiles = array.reshape(*shape[:dim], size, shape[dim] // size, *shape[dim + 1 :])
    return jnp.moveaxis(tiles, dim, 0)


def summed_on_arrival(array, axis, dim):
    size = lax.axis_size(axis)
    tiles = lax.all_to_all(in_blocks(array, dim, size), axis, 0, 0, tiled=True)
    return jnp.sum(tiles, axis=0)


def per_device(heads_concat, w_out):
    weight_half = lax.all_gather(w_out, "row", axis=0, tiled=True)
    partial_sum = jnp.dot(
        collect(heads_concat, "col", 1), weight_half, preferred_element_type=jnp.float32
    )
    summed = summed_on_arrival(partial_sum, "depth", 1)
    return summed.astype(jnp.bfloat16)


def solution(mesh):
    return jax.shard_map(
        per_device,
        mesh=mesh,
        in_specs=(P("row", ("depth", "col")), P(("depth", "row"), "col")),
        out_specs=P("row", ("col", "depth")),
        check_vma=False,
    )
```

profile of v0, /device:TPU:8, one launch (start us, length us, event | category | flops | bytes accessed | tf_op | source)
XLA Modules:
  0.0 277.6 jit_solution(3857132418449797120)
XLA Ops:
  6.5 0.0 all-gather.2.cloned.1.call-start
  6.5 0.7 all-gather.2.cloned.1.call-update
  7.3 2.3 broadcast_in_dim.3
  9.5 98.8 %all_to_all.10 = bf16[8,512,1024]{2,1,0:T(8,128)(2,1)} all-to-all(bf16[8,512,1024]{2,1,0:T(8,128)(2,1)S(1)} %broadcast_in_dim.3), channel_id=1, replica_groups=mesh['row'=16,'col'=8,'depth'=2] {'col'}, dimensions={0} | all-to-all | bytes 16777216 | tf_op jit(solution)/shard_map/all_to_all | solution.py:9
  108.4 11.4 %copy.4 = bf16[512,8,1024]{2,1,0:T(8,128)(2,1)} copy(bf16[512,8,1024]{2,0,1:T(8,128)(2,1)} %bitcast.7) | data formatting | bytes 16777216 | tf_op jit(solution)/shard_map/transpose | solution.py:13
  119.7 13.5 %reshape.6 = bf16[512,8192,1]{1,0,2:T(8,128)(2,1)} reshape(bf16[512,8,1024]{2,1,0:T(8,128)(2,1)} %copy.4) | data formatting | bytes 16777216 | tf_op jit(solution)/shard_map/reshape | solution.py:15
  133.2 79.8 %all-gather.2.cloned.1.call-done = bf16[8192,896]{1,0:T(8,128)(2,1)} async-done(((bf16[512,896]{1,0:T(8,128)(2,1)}), bf16[8192,896]{1,0:T(8,128)(2,1)}) %all-gather.2.cloned.1.call-update) | async-done | bytes 14680080 | tf_op jit(solution)/shard_map/all_gather | solution.py:36
  213.0 19.4 %copy.5 = bf16[896,8192]{1,0:T(8,128)(2,1)} copy(bf16[896,8192]{0,1:T(8,128)(2,1)} %bitcast.8) | data formatting | bytes 29360128 | tf_op jit(solution)/shard_map/dot_general | solution.py:37
  232.4 13.5 %convolution_bitcast_fusion = f32[2,512,448]{1,2,0:T(8,128)S(1)} fusion(bf16[512,8192,1]{1,0,2:T(8,128)(2,1)} %reshape.6, bf16[2,448,8192]{2,1,0:T(8,128)(2,1)} %bitcast.9), kind=kOutput, calls=%fused_computation | convolution fusion | flops 7516192768 | bytes 24903680 | tf_op jit(solution)/shard_map/dot_general | solution.py:37
  245.9 23.8 %all_to_all.11 = f32[2,512,448]{1,2,0:T(8,128)S(1)} all-to-all(f32[2,512,448]{1,2,0:T(8,128)S(1)} %convolution_bitcast_fusion), channel_id=1, replica_groups=mesh['row'=16,'col'=8,'depth'=2] {'depth'}, dimensions={0} | all-to-all | bytes 3670016 | tf_op jit(solution)/shard_map/all_to_all | solution.py:31
  269.7 1.0 reduce_sum.9
Async XLA Ops:
  6.5 206.5 %all-gather.2.cloned.1.call-start = ((), (), s32[]{:S(2)}) async-start(), calls=%async_computation.2 | async-start | bytes 15597568 | tf_op jit(solution)/shard_map/all_gather | solution.py:36
Sparse Core Ops, SparseCore 0:
  9.9 203.0 all-gather.1
where the time goes:
time: 280 us; the launch traced here: 278 us
  blocking collectives  123 us (44%)
  waiting for transfers between devices  80.5 us (29%)
  local copies, waits for them, and re-layouts  46.5 us (17%)
  matrix products  13.5 us (5%)
  between operations  13.4 us (5%)
    all_to_all x1, blocking collectives, from_everyone(): return lax.all_to_all(copies, axis, split_axis=0, concat_axis=0, tiled=True)  98.8 us
    all_gather x1, waiting for transfers between devices, per_device(): weight_half = lax.all_gather(w_out, 'row', axis=0, tiled=True)  79.8 us
    all_to_all x1, blocking collectives, summed_on_arrival(): tiles = lax.all_to_all(in_blocks(array, dim, size), axis, 0, 0, tiled=True)  23.8 us
    dot_general x1, local copies, waits for them, and re-layouts, per_device(): jnp.dot(collect(heads_concat, 'col', 1), weight_half, preferred_element_t...  19.4 us
    reshape x1, local copies, waits for them, and re-layouts, joined_along(): tiles.reshape(*shape[:dim], shape[dim] * shape[dim + 1], *shape[dim + 2:])  13.5 us
    dot_general x1, matrix products, per_device(): jnp.dot(collect(heads_concat, 'col', 1), weight_half, preferred_element_t...  13.5 us
    transpose x1, local copies, waits for them, and re-layouts, joined_along(): tiles = jnp.moveaxis(tiles, 0, dim)  11.4 us
  transfers between devices with their start and end apart: 1, of which 1 were waited for; matrix products, arithmetic and copies ran while one was open for 10% of the time, Pallas kernels for 0%

commit v1 on v0

v1 whole, which is shorter than its diff:
```python
import functools

import jax
import jax.numpy as jnp
from jax import lax
from jax.experimental import pallas as pl
from jax.experimental.pallas import tpu as pltpu
from jax.sharding import PartitionSpec as P

MESH = pl.DeviceIdType.MESH
F32 = jnp.float32
BF16 = jnp.bfloat16

Z_ORDER = (
    [(t, 0) for t in (0, 6, 1, 5)]
    + [(t, 1) for t in (0, 6, 1, 5)]
    + [(0, 2), (6, 2), (2, 0), (4, 0), (1, 2), (5, 2)]
    + [(0, 3), (6, 3), (2, 1), (4, 1), (1, 3), (5, 3), (3, 0)]
    + [(2, 2), (4, 2), (3, 1), (2, 3), (4, 3), (3, 2), (3, 3)]
)
TILE_US = 2.8
HALF_PIECE_US = 5.6
LATENCY_US = 2.2


class Plan:
    def __init__(self):
        self.steps = []

    def at(self, time, step):
        self.steps.append((time, len(self.steps), step))

    def run(self):
        for _, _, step in sorted(self.steps, key=lambda s: s[:2]):
            step()


def kernel(
    heads, w, out, a, b, c, x_out, x_fwd, packed, r_up, r_down, q_up, q_down,
    load_sem, zs, zr, xs, xr, ds, dr, es, er, ys, yr,
):
    row, col, depth = lax.axis_index("row"), lax.axis_index("col"), lax.axis_index("depth")
    z, hi, lo = row // 2, row % 2, depth
    y = hi * 2 + lo
    rows, kb = 512, 512
    half = rows // 2
    lower, upper = pl.ds(0, half), pl.ds(half, half)

    def z_peer(step):
        return (((z + 8 + step) % 8) * 2 + hi, col, depth)

    def x_peer(step):
        return (row, (col + 8 + 2 * step) % 8, depth)

    def y_at(step):
        return (y + 4 + step) % 4

    def y_peer(step):
        other = y_at(step)
        return (z * 2 + other // 2, col, other % 2)

    twin = (row, col + 1 - 2 * (col % 2), depth)
    twin_col = col + 1 - 2 * (col % 2)

    sent = []

    def send(src, dst, send_sem, recv_sem, to):
        copy = pltpu.make_async_remote_copy(
            src_ref=src, dst_ref=dst, send_sem=send_sem, recv_sem=recv_sem, device_id=to, device_id_type=MESH
        )
        copy.start()
        sent.append(copy)

    def arrived(dst, send_sem, recv_sem, frm):
        pltpu.make_async_remote_copy(
            src_ref=dst, dst_ref=dst, send_sem=send_sem, recv_sem=recv_sem, device_id=frm, device_id_type=MESH
        ).wait_recv()

    load_own = pltpu.make_async_copy(heads.at[:, pl.ds(pl.multiple_of(hi * kb, kb), kb)], a.at[col, hi], load_sem.at[0])
    load_other = pltpu.make_async_copy(heads.at[:, pl.ds(pl.multiple_of((1 - hi) * kb, kb), kb)], x_out, load_sem.at[1])
    load_w = [
        pltpu.make_async_copy(w.at[:, pl.ds(128 * t, 128)], b.at[t, z], load_sem.at[2 + t]) for t in range(7)
    ]
    own_order = [t for t, hop in Z_ORDER if hop == 0]
    load_w[own_order[0]].start()
    load_own.start()
    load_other.start()
    for t in own_order[1:]:
        load_w[t].start()

    barrier = pltpu.get_barrier_semaphore()
    peers = [z_peer(1), z_peer(-1), x_peer(1), x_peer(-1), y_peer(1), y_peer(-1), twin]
    for peer in peers:
        pl.semaphore_signal(barrier, inc=1, device_id=peer, device_id_type=MESH)
    pl.semaphore_wait(barrier, len(peers))

    plan = Plan()

    def z_view(t, origin_steps, way, split):
        block = b.at[t, (z + 8 - way * origin_steps) % 8]
        return block.at[lower if way == 1 else upper] if split else block

    def z_send(t, hop):
        for i, way in enumerate((1, -1)):
            view = z_view(t, hop, way, hop == 3)
            send(view, view, zs.at[i, t, hop], zr.at[i, t, hop], z_peer(way))

    def z_arrived(t, hop):
        for i, way in enumerate((1, -1)):
            arrived(z_view(t, hop + 1, way, hop == 3), zs.at[i, t, hop], zr.at[i, t, hop], z_peer(-way))

    def z_step(t, hop):
        if hop == 0:
            load_w[t].wait()
        else:
            z_arrived(t, hop - 1)
        z_send(t, hop)

    link_free, key, z_time = 0.0, 0.0, {}
    for t, hop in Z_ORDER:
        ready = z_time[t, hop - 1] if hop else 0.0
        key = max(key, ready)
        plan.at(key, functools.partial(z_step, t, hop))
        link_free = max(link_free, ready) + TILE_US * (0.5 if hop == 3 else 1.0)
        z_time[t, hop] = link_free + LATENCY_US

    def x_half(way, second):
        return lower if (way == 1) != second else upper

    own, other = hi, 1 - hi
    h_of = (own, other)

    def x_own(k, second):
        for i, way in enumerate((1, -1)):
            view = a.at[col, h_of[k], x_half(way, second)]
            send(view, view, xs.at[i, k, int(second)], xr.at[i, k, int(second)], x_peer(way))

    def from_x(k, i, way, part):
        steps = 1 if part < 2 else 2
        block = a.at[(col + 8 - 2 * way * steps) % 8, h_of[k]]
        return block.at[x_half(way, part == 1)]

    def x_arrived(k, part):
        for i, way in enumerate((1, -1)):
            arrived(from_x(k, i, way, part), xs.at[i, k, part], xr.at[i, k, part], x_peer(-way))

    def x_forward(k):
        x_arrived(k, 0)
        for i, way in enumerate((1, -1)):
            view = from_x(k, i, way, 0)
            send(view, view, xs.at[i, k, 2], xr.at[i, k, 2], x_peer(way))

    def twin_piece(column, k, n):
        if n == 0:
            return a.at[column, h_of[k]]
        way = 1 if n % 2 else -1
        if n <= 2:
            return a.at[(column + 8 - 2 * way) % 8, h_of[k]]
        return a.at[(column + 4) % 8, h_of[k], x_half(way, False)]

    def twin_send(k, n):
        view = twin_piece(col, k, n)
        send(view, view, ds.at[k, n], dr.at[k, n], twin)

    def twin_arrived(k, n):
        arrived(twin_piece(twin_col, k, n), ds.at[k, n], dr.at[k, n], twin)

    def own_heads():
        load_own.wait()
        x_own(0, False)
        x_own(0, True)
        twin_send(0, 0)

    def exchange():
        load_other.wait()
        send(x_out.at[lower], x_fwd.at[0], es.at[0, 0], er.at[0, 0], y_peer(1))
        send(x_out.at[upper], x_fwd.at[1], es.at[1, 0], er.at[1, 0], y_peer(-1))

    def exchange_forward():
        for i, way in enumerate((1, -1)):
            arrived(x_fwd.at[i], es.at[i, 0], er.at[i, 0], y_peer(-way))
            from_hi = y_at(-way) // 2
            send(
                x_fwd.at[i], a.at[col, from_hi, lower if way == 1 else upper], es.at[i, 1], er.at[i, 1], y_peer(way)
            )

    def exchanged():
        for i, way in enumerate((1, -1)):
            arrived(a.at[col, other, lower if way == 1 else upper], es.at[i, 1], er.at[i, 1], y_peer(-way))
        x_own(1, False)
        x_own(1, True)
        twin_send(1, 0)

    plan.at(0.0, own_heads)
    plan.at(0.0, exchange)
    e1 = HALF_PIECE_US + LATENCY_US
    plan.at(e1, exchange_forward)
    e2 = e1 + HALF_PIECE_US + LATENCY_US
    plan.at(e2, exchanged)

    def x_second(k):
        x_arrived(k, 1)
        twin_send(k, 1)
        twin_send(k, 2)

    def x_third(k):
        x_arrived(k, 2)
        twin_send(k, 3)
        twin_send(k, 4)

    def x_done(k):
        for n in range(5):
            twin_arrived(k, n)

    for k in range(2):
        x0 = 3 * k * HALF_PIECE_US + LATENCY_US
        plan.at(x0 + HALF_PIECE_US, functools.partial(x_forward, k))
        plan.at(x0 + 2 * HALF_PIECE_US, functools.partial(x_second, k))
        plan.at(x0 + 3 * HALF_PIECE_US, functools.partial(x_third, k))
        plan.at(x0 + 3 * HALF_PIECE_US + 2.0, functools.partial(x_done, k))
    heads_time = 6 * HALF_PIECE_US + LATENCY_US + 2.0

    def multiply(tiles, blocks, first):
        @pl.loop(0, 4)
        def _(i):
            h, at = i // 2, pl.ds(pl.multiple_of((i % 2) * half, half), half)
            total = None
            for k in blocks:
                index = k if len(blocks) == 8 else (z + k) % 8
                right = [b[t, index] for t in tiles]
                right = right[0] if len(tiles) == 1 else jnp.concatenate(right, axis=1)
                term = jnp.dot(a[index, h, at, :], right, preferred_element_type=F32)
                total = term if total is None else total + term
            for n, t in enumerate(tiles):
                part = total[:, 128 * n : 128 * (n + 1)]
                c[t, h, at, :] = part if first else c[t, h, at, :] + part

    pairs = ((0, 6), (1, 5), (2, 4))
    hi_up, hi_down = y_at(1) // 2, y_at(-1) // 2

    def pair_views(p):
        if p < 3:
            first, last = pairs[p]
            mine, theirs = first + lo * (last - first), last - lo * (last - first)
            return (lambda h: c.at[mine, h]), (lambda h: c.at[theirs, h]), half
        return (lambda h: packed.at[lo, h]), (lambda h: packed.at[1 - lo, h]), half // 2

    def recv(buffer, p):
        return buffer.at[p] if p < 3 else buffer.at[3, pl.ds(0, buffer.shape[1] // 2)]

    def sum_start(p):
        mine, theirs, n = pair_views(p)
        low, high = pl.ds(0, n), pl.ds(n, n)
        send(mine(other).at[low], recv(q_down, p), ys.at[p, 0], yr.at[p, 0], y_peer(1))
        send(mine(other).at[high], recv(q_up, p), ys.at[p, 1], yr.at[p, 1], y_peer(-1))
        send(theirs(hi_up).at[high], recv(r_down, p).at[high], ys.at[p, 2], yr.at[p, 2], y_peer(1))
        send(theirs(hi_down).at[low], recv(r_up, p).at[low], ys.at[p, 3], yr.at[p, 3], y_peer(-1))

    def sum_pass(p):
        _, theirs, n = pair_views(p)
        low, high = pl.ds(0, n), pl.ds(n, n)
        arrived(recv(q_down, p), ys.at[p, 0], yr.at[p, 0], y_peer(-1))
        block = theirs(hi_up).at[low]
        block[...] = block[...] + recv(q_down, p)[...]
        send(block, recv(r_down, p).at[low], ys.at[p, 4], yr.at[p, 4], y_peer(1))
        arrived(recv(q_up, p), ys.at[p, 1], yr.at[p, 1], y_peer(1))
        block = theirs(hi_down).at[high]
        block[...] = block[...] + recv(q_up, p)[...]
        send(block, recv(r_up, p).at[high], ys.at[p, 5], yr.at[p, 5], y_peer(-1))

    def sum_end(p):
        mine, _, n = pair_views(p)
        low, high = pl.ds(0, n), pl.ds(n, n)
        arrived(recv(r_down, p).at[high], ys.at[p, 2], yr.at[p, 2], y_peer(-1))
        arrived(recv(r_up, p).at[low], ys.at[p, 3], yr.at[p, 3], y_peer(1))
        arrived(recv(r_down, p).at[low], ys.at[p, 4], yr.at[p, 4], y_peer(-1))
        arrived(recv(r_up, p).at[high], ys.at[p, 5], yr.at[p, 5], y_peer(1))
        total = mine(hi)[...] + recv(r_down, p)[...] + recv(r_up, p)[...]
        total = total.astype(BF16)
        if p < 3:
            @pl.when(lo == 0)
            def _():
                out[:, 128 * p : 128 * (p + 1)] = total

            @pl.when(lo == 1)
            def _():
                start = 64 + 128 * (2 - p)
                out[:, start : start + 128] = total
        else:
            for side, start in ((0, 384), (1, 0)):
                @pl.when(lo == side)
                def _():
                    out[0:256, start : start + 64] = total[:, :64]
                    out[256:512, start : start + 64] = total[:, 64:]

    def pack():
        lane = lax.broadcasted_iota(jnp.int32, (half, 128), 1)
        for h in range(2):
            top, bottom = c[3, h, 0:half, :], c[3, h, half:rows, :]
            packed[0, h] = jnp.where(lane < 64, top, pltpu.roll(bottom, 64, 1))
            packed[1, h] = jnp.where(lane < 64, pltpu.roll(top, 64, 1), bottom)

    busy = 0.0
    for p, tiles in enumerate(pairs):
        def start(p=p, tiles=tiles):
            for t in tiles:
                z_arrived(t, 3)
            multiply(tiles, range(8), True)
            sum_start(p)

        when = max(heads_time, max(z_time[t, 3] for t in tiles))
        plan.at(when, start)
        begin = max(busy, when + 3.0)
        plan.at(begin + 2.8 + LATENCY_US, functools.partial(sum_pass, p))
        plan.at(begin + 8.4 + LATENCY_US, functools.partial(sum_end, p))
        busy = begin + 8.4

    def early():
        multiply((3,), (0, 1, 2, 3, 5, 6, 7), True)

    def late():
        z_arrived(3, 3)
        multiply((3,), (4,), False)
        pack()
        sum_start(3)
        sum_pass(3)
        sum_end(3)

    plan.at(z_time[3, 2] + 0.1, early)
    plan.at(1e9, late)

    plan.run()
    for copy in sent:
        copy.wait_send()


def solution(mesh):
    def per_device(heads, w):
        rows, features = heads.shape
        depth, columns = w.shape
        dma = pltpu.SemaphoreType.DMA
        return pl.pallas_call(
            kernel,
            out_shape=jax.ShapeDtypeStruct((rows, columns // 2), BF16),
            in_specs=[pl.BlockSpec(memory_space=pl.ANY)] * 2,
            out_specs=pl.BlockSpec(memory_space=pltpu.VMEM),
            scratch_shapes=[
                pltpu.VMEM((8, 2, 512, 512), BF16),
                pltpu.VMEM((7, 8, 512, 128), BF16),
                pltpu.VMEM((7, 2, 512, 128), F32),
                pltpu.VMEM((512, 512), BF16),
                pltpu.VMEM((2, 256, 512), BF16),
                pltpu.VMEM((2, 2, 256, 128), F32),
                pltpu.VMEM((4, 512, 128), F32),
                pltpu.VMEM((4, 512, 128), F32),
                pltpu.VMEM((4, 256, 128), F32),
                pltpu.VMEM((4, 256, 128), F32),
                dma((9,)),
                dma((2, 7, 4)),
                dma((2, 7, 4)),
                dma((2, 2, 3)),
                dma((2, 2, 3)),
                dma((2, 5)),
                dma((2, 5)),
                dma((2, 2)),
                dma((2, 2)),
                dma((4, 6)),
                dma((4, 6)),
            ],
            compiler_params=pltpu.CompilerParams(
                collective_id=0, has_side_effects=True, vmem_limit_bytes=60 * 2**20
            ),
            name="projection",
        )(heads, w)

    return jax.shard_map(
        per_device,
        mesh=mesh,
        in_specs=(P("row", ("depth", "col")), P(("depth", "row"), "col")),
        out_specs=P("row", ("col", "depth")),
        check_vma=False,
    )
```

time: 280 us -> 103 us (0.37)
  blocking collectives: 123 us -> 0 us
  Pallas kernels: 0 us -> 101 us
  waiting for transfers between devices: 80.5 us -> 0 us
  local copies, waits for them, and re-layouts: 46.5 us -> 2 us
  matrix products: 13.5 us -> 0 us
  between operations: 13.4 us -> 0.01 us
    all_to_all x2 -> x0, blocking collectives: 123 us -> none  [the longest x1 98.8 us: from_everyone(): return lax.all_to_all(copies, axis, split_axis=0, concat_axis=0, tiled=True)]
    pallas_call x0 -> x1, Pallas kernels: none -> 101 us  [per_device(): pl.pallas_call(kernel, out_shape=jax.ShapeDtypeStruct((rows, columns // 2...]
    all_gather x1 -> x0, waiting for transfers between devices: 79.8 us -> none  [per_device(): weight_half = lax.all_gather(w_out, 'row', axis=0, tiled=True)]
    dot_general x1 -> x0, local copies, waits for them, and re-layouts: 19.4 us -> none  [per_device(): jnp.dot(collect(heads_concat, 'col', 1), weight_half, preferred_element_t...]
    reshape x1 -> x0, local copies, waits for them, and re-layouts: 13.5 us -> none  [joined_along(): tiles.reshape(*shape[:dim], shape[dim] * shape[dim + 1], *shape[dim + 2:])]
    dot_general x1 -> x0, matrix products: 13.5 us -> none  [per_device(): jnp.dot(collect(heads_concat, 'col', 1), weight_half, preferred_element_t...]
    transpose x1 -> x0, local copies, waits for them, and re-layouts: 11.4 us -> none  [joined_along(): tiles = jnp.moveaxis(tiles, 0, dim)]
  transfers between devices with their start and end apart: 1 -> 0, of which waited for: 1 -> 0; matrix products, arithmetic and copies ran while one was open for 10% -> 0% of each run, Pallas kernels for 0% -> 0%
where the time goes in v1:
time: 103 us
  Pallas kernels  101 us (98%)
  local copies, waits for them, and re-layouts  2 us (2%)
    pallas_call x1, Pallas kernels, per_device(): pl.pallas_call(kernel, out_shape=jax.ShapeDtypeStruct((rows, columns // 2...  101 us

profile of v1, /device:TPU:8, one launch (start us, length us, event | category | flops | bytes accessed | tf_op | source)
XLA Modules:
  0.0 103.3 jit_solution(3890850878264745750)
XLA Ops:
  0.0 101.3 %projection.1 = bf16[512,448]{1,0:T(8,128)(2,1)} custom-call(bf16[512,1024]{1,0:T(8,128)(2,1)} %heads.1, bf16[512,896]{1,0:T(8,128)(2,1)} %w.1), custom_call_target="tpu_custom_call" | custom-call | tf_op jit(solution)/shard_map/projection/pallas_call | solution.py:342
  101.3 2.0 %copy.3 = bf16[512,448]{0,1:T(8,128)(2,1)} copy(bf16[512,448]{1,0:T(8,128)(2,1)} %projection.1) | data formatting | bytes 917504 | tf_op jit(solution)/shard_map/projection/pallas_call | solution.py:342

commit v2 on v1

v2 whole, which is shorter than its diff:
```python
import functools

import jax
import jax.numpy as jnp
from jax import lax
from jax.experimental import pallas as pl
from jax.experimental.pallas import tpu as pltpu
from jax.sharding import PartitionSpec as P

MESH = pl.DeviceIdType.MESH
F32 = jnp.float32
BF16 = jnp.bfloat16

TILES, LAST = 7, 6
Z_ORDER = (
    [(0, 0, 0), (1, 0, 0), (2, 0, 0), (3, 0, 0), (0, 1, 0), (1, 1, 0), (2, 1, 0), (3, 1, 0), (0, 2, 0), (1, 2, 0)]
    + [(4, 0, 0), (2, 2, 0), (0, 3, 0), (1, 3, 0), (3, 2, 0), (4, 1, 0), (5, 0, 0), (2, 3, 0), (3, 3, 0), (4, 2, 0)]
    + [(5, 1, 0), (6, 0, 0), (4, 3, 0), (6, 0, 1), (5, 2, 0), (6, 1, 0), (6, 1, 1), (5, 3, 0), (6, 2, 0), (6, 2, 1)]
    + [(6, 3, 0)]
)
TILE_US = 2.85
HALF_PIECE_US = 6.0
LATENCY_US = 3.0
PASS_LATE_US = 1.0
END_LATE_US = 30.0


class Plan:
    def __init__(self):
        self.steps = []

    def at(self, time, step):
        self.steps.append((time, len(self.steps), step))

    def run(self):
        for _, _, step in sorted(self.steps, key=lambda s: s[:2]):
            step()


def kernel(
    heads, w, out, a, b, w_own, x_out, x_fwd, sums, r_up, r_down, q_up, q_down,
    load_sem, zs, zr, xs, xr, ds, dr, es, er, ys, yr,
):
    row, col, depth = lax.axis_index("row"), lax.axis_index("col"), lax.axis_index("depth")
    z, hi, lo = row // 2, row % 2, depth
    y = hi * 2 + lo
    rows, kb = 512, 512
    half = rows // 2
    lower, upper = pl.ds(0, half), pl.ds(half, half)

    def z_peer(step):
        return (((z + 8 + step) % 8) * 2 + hi, col, depth)

    def x_peer(step):
        return (row, (col + 8 + 2 * step) % 8, depth)

    def y_at(step):
        return (y + 4 + step) % 4

    def y_peer(step):
        other = y_at(step)
        return (z * 2 + other // 2, col, other % 2)

    twin = (row, col + 1 - 2 * (col % 2), depth)
    twin_col = col + 1 - 2 * (col % 2)

    sent = []

    def send(src, dst, send_sem, recv_sem, to):
        copy = pltpu.make_async_remote_copy(
            src_ref=src, dst_ref=dst, send_sem=send_sem, recv_sem=recv_sem, device_id=to, device_id_type=MESH
        )
        copy.start()
        sent.append(copy)

    def arrived(dst, send_sem, recv_sem, frm):
        pltpu.make_async_remote_copy(
            src_ref=dst, dst_ref=dst, send_sem=send_sem, recv_sem=recv_sem, device_id=frm, device_id_type=MESH
        ).wait_recv()

    load_own = pltpu.make_async_copy(heads.at[:, pl.ds(pl.multiple_of(hi * kb, kb), kb)], a.at[col, hi], load_sem.at[0])
    load_other = pltpu.make_async_copy(heads.at[:, pl.ds(pl.multiple_of((1 - hi) * kb, kb), kb)], x_out, load_sem.at[1])
    load_w = [
        pltpu.make_async_copy(w.at[:, pl.ds(128 * t, 128)], w_own.at[t], load_sem.at[2 + t]) for t in range(TILES)
    ]
    for t in (0, 3, 4, 1, 5, 2, 6):
        load_w[t].start()
    load_own.start()
    load_other.start()

    barrier = pltpu.get_barrier_semaphore()
    peers = [z_peer(1), z_peer(-1), x_peer(1), x_peer(-1), y_peer(1), y_peer(-1), twin]
    for peer in peers:
        pl.semaphore_signal(barrier, inc=1, device_id=peer, device_id_type=MESH)

    loaded = set()
    lane = lax.broadcasted_iota(jnp.int32, (rows, 128), 1)
    for t in range(TILES):
        left, right = t // 2, (TILES + t) // 2
        for n in (left, right):
            if n not in loaded:
                load_w[n].wait()
                loaded.add(n)
        if t % 2 == 0:
            b[t, z] = jnp.where(lane < 64, w_own[left].astype(F32), w_own[right].astype(F32)).astype(BF16)
        else:
            both = jnp.where(lane < 64, w_own[right].astype(F32), w_own[left].astype(F32))
            b[t, z] = pltpu.roll(both, 64, 1).astype(BF16)

    pl.semaphore_wait(barrier, len(peers))

    plan = Plan()

    def z_view(t, origin_steps, way, part, split):
        block = b.at[t, (z + 8 - way * origin_steps) % 8]
        return block.at[lower if (way == 1) == (part == 0) else upper] if split else block

    def z_slot(t, part):
        return t + part * (TILES - t)

    def z_send(t, hop, part):
        slot = z_slot(t, part)
        for i, way in enumerate((1, -1)):
            view = z_view(t, hop, way, part, t == LAST or hop == 3)
            send(view, view, zs.at[i, slot, hop], zr.at[i, slot, hop], z_peer(way))

    def z_arrived(t, hop, part):
        slot = z_slot(t, part)
        for i, way in enumerate((1, -1)):
            view = z_view(t, hop + 1, way, part, t == LAST or hop == 3)
            arrived(view, zs.at[i, slot, hop], zr.at[i, slot, hop], z_peer(-way))

    def z_step(t, hop, part):
        if hop:
            z_arrived(t, hop - 1, part)
        z_send(t, hop, part)

    link_free, key, z_time = 0.0, 0.0, {}
    for t, hop, part in Z_ORDER:
        ready = z_time[t, hop - 1, part] if hop else 0.0
        key = max(key, ready)
        plan.at(key, functools.partial(z_step, t, hop, part))
        link_free = max(link_free, ready) + TILE_US * (0.5 if hop == 3 or t == LAST else 1.0)
        z_time[t, hop, part] = link_free + LATENCY_US

    def x_half(way, second):
        return lower if (way == 1) != second else upper

    own, other = hi, 1 - hi
    h_of = (own, other)

    def x_own(k, second):
        for i, way in enumerate((1, -1)):
            view = a.at[col, h_of[k], x_half(way, second)]
            send(view, view, xs.at[i, k, int(second)], xr.at[i, k, int(second)], x_peer(way))

    def from_x(k, i, way, part):
        steps = 1 if part < 2 else 2
        block = a.at[(col + 8 - 2 * way * steps) % 8, h_of[k]]
        return block.at[x_half(way, part == 1)]

    def x_arrived(k, part):
        for i, way in enumerate((1, -1)):
            arrived(from_x(k, i, way, part), xs.at[i, k, part], xr.at[i, k, part], x_peer(-way))

    def x_forward(k):
        x_arrived(k, 0)
        for i, way in enumerate((1, -1)):
            view = from_x(k, i, way, 0)
            send(view, view, xs.at[i, k, 2], xr.at[i, k, 2], x_peer(way))

    def twin_piece(column, k, n):
        if n == 0:
            return a.at[column, h_of[k]]
        way = 1 if n % 2 else -1
        if n <= 2:
            return a.at[(column + 8 - 2 * way) % 8, h_of[k]]
        return a.at[(column + 4) % 8, h_of[k], x_half(way, False)]

    def twin_send(k, n):
        view = twin_piece(col, k, n)
        send(view, view, ds.at[k, n], dr.at[k, n], twin)

    def twin_arrived(k, n):
        arrived(twin_piece(twin_col, k, n), ds.at[k, n], dr.at[k, n], twin)

    def own_heads():
        load_own.wait()
        x_own(0, False)
        x_own(0, True)
        twin_send(0, 0)

    def exchange():
        load_other.wait()
        send(x_out.at[lower], x_fwd.at[0], es.at[0, 0], er.at[0, 0], y_peer(1))
        send(x_out.at[upper], x_fwd.at[1], es.at[1, 0], er.at[1, 0], y_peer(-1))

    def exchange_forward():
        for i, way in enumerate((1, -1)):
            arrived(x_fwd.at[i], es.at[i, 0], er.at[i, 0], y_peer(-way))
            from_hi = y_at(-way) // 2
            send(
                x_fwd.at[i], a.at[col, from_hi, lower if way == 1 else upper], es.at[i, 1], er.at[i, 1], y_peer(way)
            )

    def exchanged():
        for i, way in enumerate((1, -1)):
            arrived(a.at[col, other, lower if way == 1 else upper], es.at[i, 1], er.at[i, 1], y_peer(-way))
        x_own(1, False)
        x_own(1, True)
        twin_send(1, 0)

    plan.at(0.0, own_heads)
    plan.at(0.0, exchange)
    e1 = HALF_PIECE_US + LATENCY_US
    plan.at(e1, exchange_forward)
    e2 = e1 + HALF_PIECE_US + LATENCY_US
    plan.at(e2, exchanged)

    def x_second(k):
        x_arrived(k, 1)
        twin_send(k, 1)
        twin_send(k, 2)

    def x_third(k):
        x_arrived(k, 2)
        twin_send(k, 3)
        twin_send(k, 4)

    def x_done(k):
        for n in range(5):
            twin_arrived(k, n)

    for k in range(2):
        x0 = 3 * k * HALF_PIECE_US + LATENCY_US
        plan.at(x0 + HALF_PIECE_US, functools.partial(x_forward, k))
        plan.at(x0 + 2 * HALF_PIECE_US, functools.partial(x_second, k))
        plan.at(x0 + 3 * HALF_PIECE_US, functools.partial(x_third, k))
        plan.at(x0 + 3 * HALF_PIECE_US + 2.0, functools.partial(x_done, k))
    heads_time = 6 * HALF_PIECE_US + LATENCY_US + 2.0

    def multiply(tiles, blocks, first, h=None):
        size = half // len(tiles)
        per_head = half // size

        @pl.loop(0, (1 if h is not None else 2) * per_head)
        def _(i):
            head = i // per_head if h is None else h
            start = pl.multiple_of((i % per_head) * size, size)
            top_at, bottom_at = pl.ds(start, size), pl.ds(start + half, size)
            total = None
            for k in blocks:
                index = k if len(blocks) == 8 else (z + 8 + k) % 8
                right = [b[t, index] for t in tiles]
                right = right[0] if len(tiles) == 1 else jnp.concatenate(right, axis=1)
                left = jnp.concatenate([a[index, head, top_at, :], a[index, head, bottom_at, :]], axis=0)
                term = jnp.dot(left, right, preferred_element_type=F32)
                total = term if total is None else total + term
            lanes = lax.broadcasted_iota(jnp.int32, (size, 128), 1)
            for n, t in enumerate(tiles):
                top, bottom = total[:size, 128 * n : 128 * (n + 1)], total[size:, 128 * n : 128 * (n + 1)]
                new = (
                    jnp.where(lanes < 64, top, pltpu.roll(bottom, 64, 1)),
                    jnp.where(lanes < 64, pltpu.roll(top, 64, 1), bottom),
                )
                for side in range(2):
                    sums[t, side, head, top_at] = new[side] if first else sums[t, side, head, top_at] + new[side]

    hi_up, hi_down = y_at(1) // 2, y_at(-1) // 2
    low, high = pl.ds(0, 128), pl.ds(128, 128)

    def cuts(t):
        count = 2 if t == LAST else 1
        return [(n, n * 128 // count, 128 // count) for n in range(count)]

    def sum_mine(t):
        for n, at, size in cuts(t):
            here = pl.ds(at, size)
            send(sums.at[t, lo, other, here], q_down.at[t, here], ys.at[t, n], yr.at[t, n], y_peer(1))
            send(
                sums.at[t, lo, other, pl.ds(128 + at, size)], q_up.at[t, here], ys.at[t, 2 + n], yr.at[t, 2 + n], y_peer(-1)
            )

    def sum_theirs(t):
        send(sums.at[t, 1 - lo, hi_up, high], r_down.at[t, high], ys.at[t, 4], yr.at[t, 4], y_peer(1))
        send(sums.at[t, 1 - lo, hi_down, low], r_up.at[t, low], ys.at[t, 5], yr.at[t, 5], y_peer(-1))

    def sum_pass(t):
        for n, at, size in cuts(t):
            here, there = pl.ds(at, size), pl.ds(128 + at, size)
            arrived(q_down.at[t, here], ys.at[t, n], yr.at[t, n], y_peer(-1))
            sums[t, 1 - lo, hi_up, here] = sums[t, 1 - lo, hi_up, here] + q_down[t, here]
            send(sums.at[t, 1 - lo, hi_up, here], r_down.at[t, here], ys.at[t, 6 + n], yr.at[t, 6 + n], y_peer(1))
            arrived(q_up.at[t, here], ys.at[t, 2 + n], yr.at[t, 2 + n], y_peer(1))
            sums[t, 1 - lo, hi_down, there] = sums[t, 1 - lo, hi_down, there] + q_up[t, here]
            send(sums.at[t, 1 - lo, hi_down, there], r_up.at[t, there], ys.at[t, 8 + n], yr.at[t, 8 + n], y_peer(-1))

    def sum_end(t):
        arrived(r_down.at[t, high], ys.at[t, 4], yr.at[t, 4], y_peer(-1))
        arrived(r_up.at[t, low], ys.at[t, 5], yr.at[t, 5], y_peer(1))
        for n, at, size in cuts(t):
            here, there = pl.ds(at, size), pl.ds(128 + at, size)
            arrived(r_down.at[t, here], ys.at[t, 6 + n], yr.at[t, 6 + n], y_peer(-1))
            arrived(r_up.at[t, there], ys.at[t, 8 + n], yr.at[t, 8 + n], y_peer(1))
        total = (sums[t, lo, hi] + r_down[t] + r_up[t]).T.astype(BF16)
        out[64 * t : 64 * (t + 1), 0:half] = total[:64]
        out[64 * t : 64 * (t + 1), half:rows] = total[64:]

    def tiles_whole(tiles):
        for t in tiles:
            z_arrived(t, 3, 0)
        multiply(tiles, range(8), True)
        for t in tiles:
            sum_mine(t)
            sum_theirs(t)

    def tile_early(t):
        multiply((t,), (0, 1, 2, 3, 5, 6, 7), True)

    def tile_late(t):
        z_arrived(t, 3, 0)
        multiply((t,), (4,), False, other)
        sum_mine(t)
        multiply((t,), (4,), False, own)
        sum_theirs(t)

    def last_early():
        multiply((LAST,), (0, 1, 2, 6, 7), True)

    def last_middle():
        z_arrived(LAST, 2, 1)
        multiply((LAST,), (3, 5), False)

    y_free = 0.0

    def plan_sums(t, begin):
        first = max(y_free, begin)
        plan.at(first + 1.4 + LATENCY_US + PASS_LATE_US, functools.partial(sum_pass, t))
        plan.at(first + 4.2 + LATENCY_US + END_LATE_US, functools.partial(sum_end, t))
        return first + 4.2

    for tiles in ((0, 1), (2, 3)):
        when = max(heads_time, max(z_time[t, 3, 0] for t in tiles))
        plan.at(when, functools.partial(tiles_whole, tiles))
        for t in tiles:
            y_free = plan_sums(t, when + 2.5)
    for t in (4, 5):
        plan.at(z_time[t, 2, 0] + 0.1, functools.partial(tile_early, t))
        plan.at(z_time[t, 3, 0], functools.partial(tile_late, t))
        y_free = plan_sums(t, z_time[t, 3, 0] + 0.6)
    plan.at(z_time[LAST, 1, 1] + 0.1, last_early)
    plan.at(z_time[LAST, 2, 1] + 0.1, last_middle)
    plan.at(z_time[LAST, 3, 0], functools.partial(tile_late, LAST))
    plan.at(1e9, functools.partial(sum_pass, LAST))
    plan.at(1e9, functools.partial(sum_end, LAST))

    plan.run()
    for copy in sent:
        copy.wait_send()


def solution(mesh):
    def per_device(heads, w):
        rows, features = heads.shape
        depth, columns = w.shape
        dma = pltpu.SemaphoreType.DMA
        return pl.pallas_call(
            kernel,
            out_shape=jax.ShapeDtypeStruct((columns // 2, rows), BF16),
            in_specs=[pl.BlockSpec(memory_space=pl.ANY)] * 2,
            out_specs=pl.BlockSpec(memory_space=pltpu.VMEM),
            scratch_shapes=[
                pltpu.VMEM((8, 2, 512, 512), BF16),
                pltpu.VMEM((7, 8, 512, 128), BF16),
                pltpu.VMEM((7, 512, 128), BF16),
                pltpu.VMEM((512, 512), BF16),
                pltpu.VMEM((2, 256, 512), BF16),
                pltpu.VMEM((7, 2, 2, 256, 128), F32),
                pltpu.VMEM((7, 256, 128), F32),
                pltpu.VMEM((7, 256, 128), F32),
                pltpu.VMEM((7, 128, 128), F32),
                pltpu.VMEM((7, 128, 128), F32),
                dma((9,)),
                dma((2, 8, 4)),
                dma((2, 8, 4)),
                dma((2, 2, 3)),
                dma((2, 2, 3)),
                dma((2, 5)),
                dma((2, 5)),
                dma((2, 2)),
                dma((2, 2)),
                dma((7, 10)),
                dma((7, 10)),
            ],
            compiler_params=pltpu.CompilerParams(
                collective_id=0, has_side_effects=True, vmem_limit_bytes=56_000_000
            ),
            name="projection",
        )(heads, w).T

    return jax.shard_map(
        per_device,
        mesh=mesh,
        in_specs=(P("row", ("depth", "col")), P(("depth", "row"), "col")),
        out_specs=P("row", ("col", "depth")),
        check_vma=False,
    )
```

time: 103 us -> 95.7 us (0.929)
  Pallas kernels: 101 us -> 94.3 us
  local copies, waits for them, and re-layouts: 2 us -> 0.77 us
    pallas_call x1, Pallas kernels: 101 us -> 94.3 us  [per_device(): pl.pallas_call(kernel, out_shape=jax.ShapeDtypeStruct((columns // 2, rows...]
    pallas_call x1 -> x0, local copies, waits for them, and re-layouts: 2 us -> none  [per_device(): pl.pallas_call(kernel, out_shape=jax.ShapeDtypeStruct((rows, columns // 2...]
where the time goes in v2:
time: 95.7 us; the launch traced here: 95 us
  Pallas kernels  94.3 us (99%)
    pallas_call x1, Pallas kernels, per_device(): pl.pallas_call(kernel, out_shape=jax.ShapeDtypeStruct((columns // 2, rows...  94.3 us

profile of v2, /device:TPU:8, one launch (start us, length us, event | category | flops | bytes accessed | tf_op | source)
XLA Modules:
  0.0 95.0 jit_solution(11030352527805711122)
XLA Ops:
  0.0 94.3 %projection.1 = bf16[448,512]{1,0:T(8,128)(2,1)S(1)} custom-call(bf16[512,1024]{1,0:T(8,128)(2,1)} %heads.1, bf16[512,896]{1,0:T(8,128)(2,1)} %w.1), custom_call_target="tpu_custom_call" | custom-call | tf_op jit(solution)/shard_map/projection/pallas_call | solution.py:367
  94.3 0.8 copy.4

commit v3 on v2

--- a/solution.py
+++ b/solution.py
@@ -11,18 +11,19 @@
 F32 = jnp.float32
 BF16 = jnp.bfloat16
 
-TILES, LAST = 7, 6
+TILES, LAST, SPLIT = 7, 6, (6,)
 Z_ORDER = (
-    [(0, 0, 0), (1, 0, 0), (2, 0, 0), (3, 0, 0), (0, 1, 0), (1, 1, 0), (2, 1, 0), (3, 1, 0), (0, 2, 0), (1, 2, 0)]
-    + [(4, 0, 0), (2, 2, 0), (0, 3, 0), (1, 3, 0), (3, 2, 0), (4, 1, 0), (5, 0, 0), (2, 3, 0), (3, 3, 0), (4, 2, 0)]
-    + [(5, 1, 0), (6, 0, 0), (4, 3, 0), (6, 0, 1), (5, 2, 0), (6, 1, 0), (6, 1, 1), (5, 3, 0), (6, 2, 0), (6, 2, 1)]
-    + [(6, 3, 0)]
+    (0, 0, 0), (1, 0, 0), (2, 0, 0), (3, 0, 0), (0, 1, 0), (1, 1, 0), (2, 1, 0), (3, 1, 0), (0, 2, 0), (1, 2, 0),
+    (4, 0, 0), (2, 2, 0), (0, 3, 0), (1, 3, 0), (3, 2, 0), (4, 1, 0), (5, 0, 0), (2, 3, 0), (3, 3, 0), (4, 2, 0),
+    (5, 1, 0), (6, 0, 0), (4, 3, 0), (6, 0, 1), (5, 2, 0), (6, 1, 0), (6, 1, 1), (5, 3, 0), (6, 2, 0), (6, 2, 1),
+    (6, 3, 0),
 )
+LOAD_ORDER = (0, 3, 4, 1, 5, 2, 6)
 TILE_US = 2.85
 HALF_PIECE_US = 6.0
 LATENCY_US = 3.0
 PASS_LATE_US = 1.0
-END_LATE_US = 30.0
+END_LATE_US = 9.0
 
 
 class Plan:
@@ -83,7 +84,7 @@
     load_w = [
         pltpu.make_async_copy(w.at[:, pl.ds(128 * t, 128)], w_own.at[t], load_sem.at[2 + t]) for t in range(TILES)
     ]
-    for t in (0, 3, 4, 1, 5, 2, 6):
+    for t in LOAD_ORDER:
         load_w[t].start()
     load_own.start()
     load_other.start()
@@ -95,7 +96,11 @@
 
     loaded = set()
     lane = lax.broadcasted_iota(jnp.int32, (rows, 128), 1)
-    for t in range(TILES):
+
+    packed_tiles = []
+
+    def pack_tile(t):
+        packed_tiles.append(t)
         left, right = t // 2, (TILES + t) // 2
         for n in (left, right):
             if n not in loaded:
@@ -107,6 +112,9 @@
             both = jnp.where(lane < 64, w_own[right].astype(F32), w_own[left].astype(F32))
             b[t, z] = pltpu.roll(both, 64, 1).astype(BF16)
 
+    own_order = list(dict.fromkeys(t for t, hop, part in Z_ORDER if hop == 0))
+    for t in own_order[:2]:
+        pack_tile(t)
     pl.semaphore_wait(barrier, len(peers))
 
     plan = Plan()
@@ -116,31 +124,33 @@
         return block.at[lower if (way == 1) == (part == 0) else upper] if split else block
 
     def z_slot(t, part):
-        return t + part * (TILES - t)
+        return TILES + SPLIT.index(t) if part else t
 
     def z_send(t, hop, part):
         slot = z_slot(t, part)
         for i, way in enumerate((1, -1)):
-            view = z_view(t, hop, way, part, t == LAST or hop == 3)
+            view = z_view(t, hop, way, part, t in SPLIT or hop == 3)
             send(view, view, zs.at[i, slot, hop], zr.at[i, slot, hop], z_peer(way))
 
     def z_arrived(t, hop, part):
         slot = z_slot(t, part)
         for i, way in enumerate((1, -1)):
-            view = z_view(t, hop + 1, way, part, t == LAST or hop == 3)
+            view = z_view(t, hop + 1, way, part, t in SPLIT or hop == 3)
             arrived(view, zs.at[i, slot, hop], zr.at[i, slot, hop], z_peer(-way))
 
     def z_step(t, hop, part):
         if hop:
             z_arrived(t, hop - 1, part)
         z_send(t, hop, part)
+        if hop == 0 and len(packed_tiles) < TILES:
+            pack_tile(own_order[len(packed_tiles)])
 
     link_free, key, z_time = 0.0, 0.0, {}
     for t, hop, part in Z_ORDER:
         ready = z_time[t, hop - 1, part] if hop else 0.0
         key = max(key, ready)
         plan.at(key, functools.partial(z_step, t, hop, part))
-        link_free = max(link_free, ready) + TILE_US * (0.5 if hop == 3 or t == LAST else 1.0)
+        link_free = max(link_free, ready) + TILE_US * (0.5 if hop == 3 or t in SPLIT else 1.0)
         z_time[t, hop, part] = link_free + LATENCY_US
 
     def x_half(way, second):
@@ -315,7 +325,12 @@
             sum_theirs(t)
 
     def tile_early(t):
-        multiply((t,), (0, 1, 2, 3, 5, 6, 7), True)
+        multiply((t,), (0, 1, 2, 6, 7), True)
+
+    def tile_middle(t):
+        if t in SPLIT:
+            z_arrived(t, 2, 1)
+        multiply((t,), (3, 5), False)
 
     def tile_late(t):
         z_arrived(t, 3, 0)
@@ -324,19 +339,12 @@
         multiply((t,), (4,), False, own)
         sum_theirs(t)
 
-    def last_early():
-        multiply((LAST,), (0, 1, 2, 6, 7), True)
-
-    def last_middle():
-        z_arrived(LAST, 2, 1)
-        multiply((LAST,), (3, 5), False)
-
     y_free = 0.0
 
     def plan_sums(t, begin):
         first = max(y_free, begin)
         plan.at(first + 1.4 + LATENCY_US + PASS_LATE_US, functools.partial(sum_pass, t))
-        plan.at(first + 4.2 + LATENCY_US + END_LATE_US, functools.partial(sum_end, t))
+        plan.at(first + 4.2 + LATENCY_US + END_LATE_US if t < 4 else 2e9, functools.partial(sum_end, t))
         return first + 4.2
 
     for tiles in ((0, 1), (2, 3)):
@@ -344,15 +352,18 @@
         plan.at(when, functools.partial(tiles_whole, tiles))
         for t in tiles:
             y_free = plan_sums(t, when + 2.5)
-    for t in (4, 5):
-        plan.at(z_time[t, 2, 0] + 0.1, functools.partial(tile_early, t))
-        plan.at(z_time[t, 3, 0], functools.partial(tile_late, t))
-        y_free = plan_sums(t, z_time[t, 3, 0] + 0.6)
-    plan.at(z_time[LAST, 1, 1] + 0.1, last_early)
-    plan.at(z_time[LAST, 2, 1] + 0.1, last_middle)
-    plan.at(z_time[LAST, 3, 0], functools.partial(tile_late, LAST))
+    for t in (4, 5, 6):
+        last_part = int(t in SPLIT)
+        key = max(z_time[t, 1, last_part], heads_time + 3.0) + 0.1
+        plan.at(key, functools.partial(tile_early, t))
+        key = max(key, z_time[t, 2, last_part]) + 0.1
+        plan.at(key, functools.partial(tile_middle, t))
+        key = max(key, z_time[t, 3, 0]) + 0.1
+        plan.at(key, functools.partial(tile_late, t))
+        if t != LAST:
+            y_free = plan_sums(t, key + 0.6)
     plan.at(1e9, functools.partial(sum_pass, LAST))
-    plan.at(1e9, functools.partial(sum_end, LAST))
+    plan.at(3e9, functools.partial(sum_end, LAST))
 
     plan.run()
     for copy in sent:
@@ -381,8 +392,8 @@
                 pltpu.VMEM((7, 128, 128), F32),
                 pltpu.VMEM((7, 128, 128), F32),
                 dma((9,)),
-                dma((2, 8, 4)),
-                dma((2, 8, 4)),
+                dma((2, 10, 4)),
+                dma((2, 10, 4)),
                 dma((2, 2, 3)),
                 dma((2, 2, 3)),
                 dma((2, 5)),

time: 95.7 us -> 92.5 us (0.967)
  Pallas kernels: 94.3 us -> 91.6 us
    pallas_call x1, Pallas kernels: 94.3 us -> 91.6 us  [per_device(): pl.pallas_call(kernel, out_shape=jax.ShapeDtypeStruct((columns // 2, rows...]
where the time goes in v3:
time: 92.5 us; the launch traced here: 92.4 us
  Pallas kernels  91.6 us (99%)
    pallas_call x1, Pallas kernels, per_device(): pl.pallas_call(kernel, out_shape=jax.ShapeDtypeStruct((columns // 2, rows...  91.6 us

profile of v3, /device:TPU:8, one launch (start us, length us, event | category | flops | bytes accessed | tf_op | source)
XLA Modules:
  0.0 92.4 jit_solution(6780376216676681310)
XLA Ops:
  0.0 91.6 %projection.1 = bf16[448,512]{1,0:T(8,128)(2,1)S(1)} custom-call(bf16[512,1024]{1,0:T(8,128)(2,1)} %heads.1, bf16[512,896]{1,0:T(8,128)(2,1)} %w.1), custom_call_target="tpu_custom_call" | custom-call | tf_op jit(solution)/shard_map/projection/pallas_call | solution.py:378
  91.6 0.8 copy.4

commit v4 on v3

--- a/solution.py
+++ b/solution.py
@@ -15,9 +15,10 @@
 Z_ORDER = (
     (0, 0, 0), (1, 0, 0), (2, 0, 0), (3, 0, 0), (0, 1, 0), (1, 1, 0), (2, 1, 0), (3, 1, 0), (0, 2, 0), (1, 2, 0),
     (4, 0, 0), (2, 2, 0), (0, 3, 0), (1, 3, 0), (3, 2, 0), (4, 1, 0), (5, 0, 0), (2, 3, 0), (3, 3, 0), (4, 2, 0),
-    (5, 1, 0), (6, 0, 0), (4, 3, 0), (6, 0, 1), (5, 2, 0), (6, 1, 0), (6, 1, 1), (5, 3, 0), (6, 2, 0), (6, 2, 1),
-    (6, 3, 0),
+    (5, 1, 0), (6, 0, 0), (6, 0, 1), (6, 0, 2), (6, 0, 3), (4, 3, 0), (5, 2, 0), (6, 1, 0), (6, 1, 1), (6, 1, 2),
+    (6, 1, 3), (6, 2, 0), (6, 2, 1), (5, 3, 0), (6, 2, 2), (6, 2, 3), (6, 3, 0), (6, 3, 1),
 )
+PARTS = 4
 LOAD_ORDER = (0, 3, 4, 1, 5, 2, 6)
 TILE_US = 2.85
 HALF_PIECE_US = 6.0
@@ -119,38 +120,50 @@
 
     plan = Plan()
 
-    def z_view(t, origin_steps, way, part, split):
+    def z_view(t, origin_steps, way, part, hop):
         block = b.at[t, (z + 8 - way * origin_steps) % 8]
-        return block.at[lower if (way == 1) == (part == 0) else upper] if split else block
+        if t in SPLIT:
+            size = rows // PARTS
+            at = part * size
+            return block.at[pl.ds(at if way == 1 else (at + half) % rows, size)]
+        return block.at[lower if way == 1 else upper] if hop == 3 else block
 
     def z_slot(t, part):
-        return TILES + SPLIT.index(t) if part else t
-
-    def z_send(t, hop, part):
+        return TILES - 1 + part if part else t
+
+    def z_send(t, hop, part, i, way):
         slot = z_slot(t, part)
-        for i, way in enumerate((1, -1)):
-            view = z_view(t, hop, way, part, t in SPLIT or hop == 3)
-            send(view, view, zs.at[i, slot, hop], zr.at[i, slot, hop], z_peer(way))
-
-    def z_arrived(t, hop, part):
+        view = z_view(t, hop, way, part, hop)
+        send(view, view, zs.at[i, slot, hop], zr.at[i, slot, hop], z_peer(way))
+
+    def z_arrived_one(t, hop, part, i, way):
         slot = z_slot(t, part)
-        for i, way in enumerate((1, -1)):
-            view = z_view(t, hop + 1, way, part, t in SPLIT or hop == 3)
-            arrived(view, zs.at[i, slot, hop], zr.at[i, slot, hop], z_peer(-way))
+        view = z_view(t, hop + 1, way, part, hop)
+        arrived(view, zs.at[i, slot, hop], zr.at[i, slot, hop], z_peer(-way))
+
+    def z_arrived(t, hop, parts):
+        for part in parts:
+            for i, way in enumerate((1, -1)):
+                z_arrived_one(t, hop, part, i, way)
 
     def z_step(t, hop, part):
-        if hop:
-            z_arrived(t, hop - 1, part)
-        z_send(t, hop, part)
+        for i, way in enumerate((1, -1)):
+            if hop:
+                z_arrived_one(t, hop - 1, part, i, way)
+            z_send(t, hop, part, i, way)
         if hop == 0 and len(packed_tiles) < TILES:
             pack_tile(own_order[len(packed_tiles)])
 
-    link_free, key, z_time = 0.0, 0.0, {}
+    def parts_of(t, hop):
+        return range(PARTS // (2 if hop == 3 else 1)) if t in SPLIT else (0,)
+
+    link_free, key, z_time, z_key = 0.0, 0.0, {}, {}
     for t, hop, part in Z_ORDER:
         ready = z_time[t, hop - 1, part] if hop else 0.0
         key = max(key, ready)
+        z_key[t, hop, part] = key
         plan.at(key, functools.partial(z_step, t, hop, part))
-        link_free = max(link_free, ready) + TILE_US * (0.5 if hop == 3 or t in SPLIT else 1.0)
+        link_free = max(link_free, ready) + TILE_US * (1.0 / PARTS if t in SPLIT else 0.5 if hop == 3 else 1.0)
         z_time[t, hop, part] = link_free + LATENCY_US
 
     def x_half(way, second):
@@ -318,7 +331,7 @@
 
     def tiles_whole(tiles):
         for t in tiles:
-            z_arrived(t, 3, 0)
+            z_arrived(t, 3, (0,))
         multiply(tiles, range(8), True)
         for t in tiles:
             sum_mine(t)
@@ -329,11 +342,11 @@
 
     def tile_middle(t):
         if t in SPLIT:
-            z_arrived(t, 2, 1)
+            z_arrived(t, 2, range(PARTS // 2, PARTS))
         multiply((t,), (3, 5), False)
 
     def tile_late(t):
-        z_arrived(t, 3, 0)
+        z_arrived(t, 3, parts_of(t, 3))
         multiply((t,), (4,), False, other)
         sum_mine(t)
         multiply((t,), (4,), False, own)
@@ -353,12 +366,12 @@
         for t in tiles:
             y_free = plan_sums(t, when + 2.5)
     for t in (4, 5, 6):
-        last_part = int(t in SPLIT)
-        key = max(z_time[t, 1, last_part], heads_time + 3.0) + 0.1
+        last_part = parts_of(t, 2)[-1]
+        key = max(z_time[t, 1, last_part], z_key[t, 2, last_part], heads_time + 3.0) + 0.1
         plan.at(key, functools.partial(tile_early, t))
-        key = max(key, z_time[t, 2, last_part]) + 0.1
+        key = max(key, z_time[t, 2, last_part], z_key[t, 3, parts_of(t, 3)[-1]]) + 0.1
         plan.at(key, functools.partial(tile_middle, t))
-        key = max(key, z_time[t, 3, 0]) + 0.1
+        key = max(key, z_time[t, 3, parts_of(t, 3)[-1]]) + 0.1
         plan.at(key, functools.partial(tile_late, t))
         if t != LAST:
             y_free = plan_sums(t, key + 0.6)

time: 92.5 us -> 92.5 us (level)
  no operation moved by 1% of the time
where the time goes in v4:
time: 92.5 us; the launch traced here: 92.4 us
  Pallas kernels  91.6 us (99%)
    pallas_call x1, Pallas kernels, per_device(): pl.pallas_call(kernel, out_shape=jax.ShapeDtypeStruct((columns // 2, rows...  91.6 us

profile of v4, /device:TPU:8, one launch (start us, length us, event | category | flops | bytes accessed | tf_op | source)
XLA Modules:
  0.0 92.4 jit_solution(3959420921962281028)
XLA Ops:
  0.0 91.6 %projection.1 = bf16[448,512]{1,0:T(8,128)(2,1)S(1)} custom-call(bf16[512,1024]{1,0:T(8,128)(2,1)} %heads.1, bf16[512,896]{1,0:T(8,128)(2,1)} %w.1), custom_call_target="tpu_custom_call" | custom-call | tf_op jit(solution)/shard_map/projection/pallas_call | solution.py:391
  91.6 0.8 copy.4

commit v5 on v4

--- a/solution.py
+++ b/solution.py
@@ -15,10 +15,10 @@
 Z_ORDER = (
     (0, 0, 0), (1, 0, 0), (2, 0, 0), (3, 0, 0), (0, 1, 0), (1, 1, 0), (2, 1, 0), (3, 1, 0), (0, 2, 0), (1, 2, 0),
     (4, 0, 0), (2, 2, 0), (0, 3, 0), (1, 3, 0), (3, 2, 0), (4, 1, 0), (5, 0, 0), (2, 3, 0), (3, 3, 0), (4, 2, 0),
-    (5, 1, 0), (6, 0, 0), (6, 0, 1), (6, 0, 2), (6, 0, 3), (4, 3, 0), (5, 2, 0), (6, 1, 0), (6, 1, 1), (6, 1, 2),
-    (6, 1, 3), (6, 2, 0), (6, 2, 1), (5, 3, 0), (6, 2, 2), (6, 2, 3), (6, 3, 0), (6, 3, 1),
+    (5, 1, 0), (6, 0, 0), (6, 0, 1), (4, 3, 0), (5, 2, 0), (6, 1, 0), (6, 1, 1), (6, 2, 0), (5, 3, 0), (6, 2, 1),
+    (6, 3, 0),
 )
-PARTS = 4
+PARTS = 2
 LOAD_ORDER = (0, 3, 4, 1, 5, 2, 6)
 TILE_US = 2.85
 HALF_PIECE_US = 6.0

time: 92.5 us -> 92.5 us (level)
  no operation moved by 1% of the time
where the time goes in v5:
time: 92.5 us; the launch traced here: 92.4 us
  Pallas kernels  91.6 us (99%)
    pallas_call x1, Pallas kernels, per_device(): pl.pallas_call(kernel, out_shape=jax.ShapeDtypeStruct((columns // 2, rows...  91.6 us

profile of v5, /device:TPU:8, one launch (start us, length us, event | category | flops | bytes accessed | tf_op | source)
XLA Modules:
  0.0 92.4 jit_solution(15317289133688738394)
XLA Ops:
  0.0 91.6 %projection.1 = bf16[448,512]{1,0:T(8,128)(2,1)S(1)} custom-call(bf16[512,1024]{1,0:T(8,128)(2,1)} %heads.1, bf16[512,896]{1,0:T(8,128)(2,1)} %w.1), custom_call_target="tpu_custom_call" | custom-call | tf_op jit(solution)/shard_map/projection/pallas_call | solution.py:391
  91.6 0.8 copy.4
